TPU v7x, 32 devices: a whole 2x2x4 slice. The times are simulated.
32 devices in a mesh: groups: 2 (over y), det: 4 (over z), blk: 2 (over x), sub: 2 (over core).
Axes of the slice: x: 2, y: 2, z: 4, core: 2. Of those that a mesh axis runs over, the one named last changes fastest.
Arguments:
- tod: float32 [256, 4, 1024], P(('groups', 'det'), None, ('blk', 'sub')), parts along dimension 0, may hold values from -30 to 30
- pixels: int32 [256, 4, 1024], P('groups', 'det', ('blk', 'sub')), parts along dimension 0, may hold values from 0 to 3071
- span_block: int32 [8, 8], P('groups', ('blk', 'sub')), parts along dimension 0, may hold values from 0 to 7
- weight_class: int32 [256], P('groups'), parts along dimension 0, may hold values from 0 to 7
- class_weight: float32 [16], P('groups'), parts along dimension 0, may hold values from 0.25 to 4
Outputs:
- signal_sum: float32 [16, 3072], P(('groups', 'blk'), ('det', 'sub')), parts along dimension 0
- weight_sum: float32 [16, 3072], P(('groups', 'blk'), ('det', 'sub')), parts along dimension 0
- hit_count: float32 [16, 3072], P(('groups', 'blk'), ('det', 'sub')), parts along dimension 0
There are 2 independent parts, one for each index of `groups`. A program takes and returns all parts, laid end to end along the dimension named above; each array names one. Nothing has to cross between parts.
All inputs are finite; a program needn't handle non-finite values.
Results may differ from a plain program's by a relative error of at most 0.005.
Values sent between devices are 32-bit elements; how exact they have to be, the bound alone decides.
A program may use at most 64 MiB of HBM per device.

v0:
```python
import functools

import jax
import jax.numpy as jnp
from jax import lax
from jax.experimental import pallas as pl
from jax.experimental.pallas import tpu as pltpu
from jax.sharding import PartitionSpec as P

BLOCK_PIX = 3072
SPAN = 128
BLK_OWN = 4
TILE = 8
PACK = 16
MESH = pl.DeviceIdType.MESH


def kernel(
    sizes,
    tod_hbm,
    pix_hbm,
    class_hbm,
    class_weight_hbm,
    span_block_hbm,
    out_ref,
    class_ref,
    class_weight_ref,
    span_block_ref,
    tod_in,
    pix_in,
    stage,
    tod_all,
    high_ref,
    low_ref,
    fine_high_ref,
    fine_low_ref,
    weight_rows,
    value_ref,
    early_out,
    early_in,
    late_out,
    late_in,
    load_sem,
    tod_send,
    tod_recv,
    early_send,
    early_recv,
    late_send,
    late_recv,
    passed,
):
    ndet, nblk, nsub, spans, lanes, rows = sizes
    peers = ndet * nsub
    total_peers = peers * nblk
    mine = tod_hbm.shape[0]
    detectors = ndet * mine
    classes = class_weight_hbm.shape[0]
    det = lax.axis_index("det")
    blk = lax.axis_index("blk")
    sub = lax.axis_index("sub")
    others = [
        (db, dd, ds)
        for dd in range(ndet)
        for db in range(nblk)
        for ds in range(nsub)
        if (db, dd, ds) != (0, 0, 0)
    ]

    def target(offset):
        db, dd, ds = offset
        return {
            "det": lax.rem(det + dd, ndet),
            "blk": lax.rem(blk + db, nblk),
            "sub": lax.rem(sub + ds, nsub),
        }

    barrier = pltpu.get_barrier_semaphore()
    plane = [offset for offset in others if offset[1] == 0]
    column = [offset for offset in others if offset[0] == 0 and offset[2] == 0]
    for offset in plane + column:
        pl.semaphore_signal(barrier, inc=1, device_id=target(offset), device_id_type=MESH)

    sources = (tod_hbm, pix_hbm, class_hbm, class_weight_hbm, span_block_hbm)
    landings = (tod_in, pix_in, class_ref, class_weight_ref, span_block_ref)
    loads = [
        pltpu.make_async_copy(source, landing, load_sem.at[n])
        for n, (source, landing) in enumerate(zip(sources, landings))
    ]
    for load in loads:
        load.start()

    part = mine * spans
    loads[0].wait()
    for seg in range(ndet):
        for span in range(spans):
            stage[seg, pl.ds(span, mine, spans), :] = tod_in[:, seg, span * SPAN : (span + 1) * SPAN]

    loads[2].wait()
    loads[3].wait()
    picked = jnp.zeros((1, detectors), jnp.float32)
    for c in range(classes):
        picked = jnp.where(class_ref[...] == c, class_weight_ref[c], picked)
    total = jnp.sum(picked, axis=1, keepdims=True)
    turned = jnp.transpose(jnp.broadcast_to(picked, (SPAN, detectors)))
    for span in range(spans):
        weight_rows[pl.ds(span, detectors, spans), :] = turned

    loads[1].wait()
    pixel = pix_in[...].astype(jnp.float32)
    high = jnp.floor((pixel + 0.5) * (1.0 / lanes))
    high_ref[...] = high
    low = pixel - high * lanes
    low_ref[...] = low
    upper = jnp.where(low >= lanes // 2, 1.0, 0.0)
    fine_high_ref[...] = 2.0 * high + upper
    fine_low_ref[...] = low - upper * (lanes // 2)

    pl.semaphore_wait(barrier, len(plane + column))
    for offset in plane:
        pl.semaphore_signal(passed, inc=1, device_id=target(offset), device_id_type=MESH)
    for step in range(1, ndet):
        seg = lax.rem(det + step, ndet)
        pltpu.make_async_remote_copy(
            src_ref=stage.at[seg],
            dst_ref=tod_all.at[det],
            send_sem=tod_send,
            recv_sem=tod_recv,
            device_id={"det": seg},
            device_id_type=MESH,
        ).start()
    tod_all[det] = stage[det]
    height = peers * TILE
    fine = lanes // 2
    fine_rows = 2 * rows
    field = SPAN // spans
    low_tiles = -(-lanes // PACK)

    def iota(tile):
        return lax.broadcasted_iota(jnp.int32, (PACK, SPAN), 0) + tile * PACK

    def to_low(x):
        return x.astype(jnp.float32).astype(jnp.bfloat16)

    low_ids = [to_low(iota(t)) for t in range(SPAN // PACK)]
    early_ids = []
    late_ids = []
    for t in range(height // PACK):
        row = iota(t)
        peer = row // TILE
        within = row % TILE
        kind = jnp.where(within < rows, within, within - rows)
        early_ids.append(to_low(jnp.where(within < 2 * rows, peer * rows + kind, -1)))
    for t in range(height // PACK):
        row = iota(t)
        within = row % TILE
        late_ids.append(to_low(jnp.where(within < fine_rows, row // TILE * fine_rows + within, -1)))
    is_weight = to_low(jnp.where(iota(0) % TILE < rows, 1, 0)) > 0.5
    one = jnp.ones((PACK, SPAN), jnp.bfloat16)
    zero = jnp.zeros((PACK, SPAN), jnp.bfloat16)

    def spread(ref, row):
        return jnp.broadcast_to(ref[pl.ds(row, 1), :], (PACK, SPAN)).astype(jnp.bfloat16)

    def hot(ids, where, filled):
        return jnp.concatenate([jnp.where(i == where, filled, zero) for i in ids], axis=0)

    chunk = min(64, detectors)

    def contract(left, right):
        return lax.dot_general(
            jnp.concatenate(left, axis=1),
            jnp.concatenate(right, axis=1),
            (((1,), (1,)), ((), ())),
            preferred_element_type=jnp.float32,
        )

    def early_step(i, sums):
        base = pl.multiple_of(i * chunk * spans, TILE)
        new = []
        for span in range(spans):
            left, right = [], []
            for d in range(chunk):
                r = base + d * spans + span
                right.append(hot(low_ids, spread(low_ref, r), one))
                filled = jnp.where(is_weight, spread(weight_rows, r), one)
                left.append(hot(early_ids, spread(high_ref, r), filled))
            new.append(sums[span] + contract(left, right))
        return tuple(new)

    start = tuple(jnp.zeros((height, SPAN), jnp.float32) for _ in range(spans))
    sums = lax.fori_loop(0, detectors // chunk, early_step, start)
    loads[4].wait()
    label_row = lax.broadcasted_iota(jnp.int32, (TILE, SPAN), 0) == 2 * rows
    for span in range(spans):
        label = span_block_ref[span, det].astype(jnp.float32)
        for p in range(peers):
            tile = sums[span][p * TILE : (p + 1) * TILE]
            early_out[p, span] = jnp.where(label_row, label, tile)

    slot_of = {offset: n for n, offset in enumerate(others)}

    def send(source, landing, send_sem, recv_sem):
        for offset in others:
            to = target(offset)
            pltpu.make_async_remote_copy(
                src_ref=source.at[to["det"] * nsub + to["sub"]],
                dst_ref=landing.at[slot_of[offset]],
                send_sem=send_sem,
                recv_sem=recv_sem,
                device_id=to,
                device_id_type=MESH,
            ).start()

    own_place = det * nsub + sub
    remote = len(others)

    pl.semaphore_wait(passed, len(plane))
    send(early_out, early_in, early_send, early_recv)

    tod_gone = stage.at[pl.ds(0, ndet - 1)]
    pltpu.make_async_copy(tod_gone, tod_all.at[pl.ds(0, ndet - 1)], tod_recv).wait()

    period = TILE
    folded = jnp.zeros((period, SPAN), jnp.float32)
    for q in range(ndet):
        weighted = tod_all[q] * weight_rows[q * part : (q + 1) * part]
        for k in range(part // period):
            folded = folded + weighted[k * period : (k + 1) * period]
    shift = spans
    while shift < period:
        folded = folded + pltpu.roll(folded, shift, 0)
        shift *= 2
    common = folded / total
    for q in range(ndet):
        piece = slice(q * part, (q + 1) * part)
        repeated = jnp.concatenate([common] * (part // period), axis=0)
        value_ref[piece] = weight_rows[piece] * (tod_all[q] - repeated)

    def late_step(i, sums):
        base = pl.multiple_of(i * chunk * spans, TILE)
        new = []
        for span in range(spans):
            left, right = [], []
            for d in range(chunk):
                r = base + d * spans + span
                right.append(hot(low_ids[: field // PACK], spread(fine_low_ref, r), one))
                left.append(hot(late_ids, spread(fine_high_ref, r), spread(value_ref, r)))
            new.append(sums[span] + contract(left, right))
        return tuple(new)

    start = tuple(jnp.zeros((height, field), jnp.float32) for _ in range(spans))
    late = lax.fori_loop(0, detectors // chunk, late_step, start)
    for p in range(peers):
        tiles = [late[span][p * TILE : (p + 1) * TILE] for span in range(spans)]
        late_out[p] = jnp.concatenate(tiles, axis=1)
    send(late_out, late_in, late_send, late_recv)
    late_in[remote] = late_out[own_place]
    early_in[remote] = early_out[own_place]

    pltpu.make_async_copy(early_in.at[pl.ds(0, remote)], early_in.at[pl.ds(0, remote)], early_recv).wait()
    first = (blk * BLK_OWN).astype(jnp.float32)

    def gather_early(n, acc):
        acc = list(acc)
        for span in range(spans):
            tile = early_in[n, span]
            label = jnp.broadcast_to(early_in[n, span, pl.ds(2 * rows, 1), :], (TILE, SPAN))
            for b in range(BLK_OWN):
                acc[b] = acc[b] + jnp.where(label == first + b, tile, 0.0)
        return tuple(acc)

    lane = lax.broadcasted_iota(jnp.int32, (TILE, SPAN), 1)

    def gather_late(n, acc):
        label = jnp.broadcast_to(early_in[n, 0, pl.ds(2 * rows, 1), :], (TILE, SPAN))
        for span in range(1, spans):
            other = jnp.broadcast_to(early_in[n, span, pl.ds(2 * rows, 1), :], (TILE, SPAN))
            label = jnp.where(lane < span * field, label, other)
        tile = late_in[n]
        return tuple(
            acc[b] + jnp.where(label == first + b, tile, 0.0) for b in range(BLK_OWN)
        )

    def over_slots(step):
        acc = tuple(jnp.zeros((TILE, SPAN), jnp.float32) for _ in range(BLK_OWN))
        if total_peers <= 16:
            for n in range(total_peers):
                acc = step(n, acc)
            return acc
        return lax.fori_loop(0, total_peers, step, acc)

    acc = over_slots(gather_early)
    for b in range(BLK_OWN):
        for r in range(rows):
            at = slice(r * lanes, (r + 1) * lanes)
            out_ref[1, b : b + 1, at] = acc[b][r : r + 1, :lanes]
            out_ref[2, b : b + 1, at] = acc[b][rows + r : rows + r + 1, :lanes]

    pltpu.make_async_copy(late_in.at[pl.ds(0, remote)], late_in.at[pl.ds(0, remote)], late_recv).wait()
    acc = over_slots(gather_late)
    for b in range(BLK_OWN):
        whole = acc[b]
        for span in range(1, spans):
            whole = whole + pltpu.roll(acc[b], span * field, 1)
        for r in range(fine_rows):
            skip = r * fine % SPAN // field * field
            skip = skip if skip + fine <= SPAN else 0
            line = whole[r : r + 1, skip : skip + fine]
            out_ref[0, b : b + 1, r * fine : (r + 1) * fine] = line

    pltpu.make_async_copy(tod_gone, tod_all.at[pl.ds(0, ndet - 1)], tod_send).wait()
    pltpu.make_async_copy(early_in.at[pl.ds(0, remote)], early_in.at[pl.ds(0, remote)], early_send).wait()
    pltpu.make_async_copy(late_in.at[pl.ds(0, remote)], late_in.at[pl.ds(0, remote)], late_send).wait()


def on_device(tod, pixels, span_block, weight_class, class_weight):
    ndet, nblk, nsub = (lax.axis_size(a) for a in ("det", "blk", "sub"))
    mine, segments, samples = tod.shape
    detectors = pixels.shape[0]
    spans = samples // SPAN
    peers = ndet * nsub
    slots = peers * nblk
    width = BLOCK_PIX // peers
    lanes = next(n for n in range(SPAN, 0, -1) if width % n == 0)
    rows = width // lanes
    assert segments == ndet and detectors == ndet * mine
    assert TILE % spans == 0 and 2 * rows < TILE and lanes % 2 == 0 and lanes // 2 <= SPAN // spans
    flat = (detectors * spans, SPAN)
    vmem = pl.BlockSpec(memory_space=pltpu.VMEM)
    hbm = pl.BlockSpec(memory_space=pl.ANY)
    f32 = jnp.float32
    dma = pltpu.SemaphoreType.DMA
    out = pl.pallas_call(
        functools.partial(kernel, (ndet, nblk, nsub, spans, lanes, rows)),
        out_shape=pltpu.VMEM((3, BLK_OWN, width), f32),
        in_specs=[hbm] * 5,
        out_specs=vmem,
        scratch_shapes=[
            pltpu.VMEM((1, detectors), jnp.int32),
            pltpu.SMEM(class_weight.shape, f32),
            pltpu.SMEM((spans, segments), jnp.int32),
            pltpu.VMEM(tod.shape, f32),
            pltpu.VMEM(flat, jnp.int32),
            pltpu.VMEM((ndet, mine * spans, SPAN), f32),
            pltpu.VMEM((ndet, mine * spans, SPAN), f32),
            pltpu.VMEM(flat, f32),
            pltpu.VMEM(flat, f32),
            pltpu.VMEM(flat, f32),
            pltpu.VMEM(flat, f32),
            pltpu.VMEM(flat, f32),
            pltpu.VMEM(flat, f32),
            pltpu.VMEM((peers, spans, TILE, SPAN), f32),
            pltpu.VMEM((slots, spans, TILE, SPAN), f32),
            pltpu.VMEM((peers, TILE, SPAN), f32),
            pltpu.VMEM((slots, TILE, SPAN), f32),
            dma((5,)),
            dma,
            dma,
            dma,
            dma,
            dma,
            dma,
            pltpu.SemaphoreType.REGULAR,
        ],
        compiler_params=pltpu.CompilerParams(collective_id=0, has_side_effects=True),
    )(
        tod,
        pixels.reshape(flat),
        weight_class.reshape(1, detectors),
        class_weight,
        span_block.T,
    )
    return (out[0], out[1], out[2])


def solution(mesh):
    placed = (
        P(("groups", "det"), None, ("blk", "sub")),
        P("groups", "det", ("blk", "sub")),
        P("groups", ("blk", "sub")),
        P("groups"),
        P("groups"),
    )
    sliced = P(("groups", "blk"), ("det", "sub"))
    return jax.shard_map(
        on_device,
        mesh=mesh,
        in_specs=placed,
        out_specs=(sliced, sliced, sliced),
        check_vma=False,
    )
```

profile of v0, /device:TPU:0, one launch (start us, length us, event | category | flops | bytes accessed | tf_op | source)
XLA Modules:
  0.0 17.4 jit_solution(2608787938999089473)
XLA Ops:
  0.6 16.1 %shard_map.76 = f32[3,4,384]{2,1,0:T(4,128)S(1)} custom-call(f32[32,4,256]{2,1,0:T(4,128)} %tod_hbm.1, s32[256,128]{1,0:T(8,128)} %bitcast.9, s32[1,128]{1,0:T(1,128)} %bitcast.11, f32[8]{0:T(128)} %class_weight_hbm.1, s32[2,4]{1,0:T(2,128)} %bitcast.10), custom_call_target="tpu_custom_call" | custom-call | tf_op jit(solution)/shard_map/pallas_call | solution.py:333
  16.8 0.6 %slice_bitcast_fusion = (f32[4,384]{1,0:T(4,128)}, f32[4,384]{1,0:T(4,128)}, f32[4,384]{1,0:T(4,128)}) fusion(f32[3,4,384]{2,1,0:T(4,128)S(1)} %shard_map.76), kind=kLoop, calls=%fused_computation | loop fusion | bytes 36864 | tf_op jit(solution)/shard_map/squeeze | solution.py:373
where the time goes:
time: 17.5 us; the launch traced here: 17.4 us
  Pallas kernels  16.1 us (92%)
  between operations  0.64 us (4%)
  local copies, waits for them, and re-layouts  0.6 us (3%)
    pallas_call x1, Pallas kernels, on_device(): pl.pallas_call(functools.partial(kernel, (ndet, nblk, nsub, spans, lanes,...  16.1 us
    squeeze x1, local copies, waits for them, and re-layouts, on_device(): return (out[0], out[1], out[2])  0.6 us

commit v1 on v0

--- a/solution.py
+++ b/solution.py
@@ -48,6 +48,7 @@
     late_send,
     late_recv,
     passed,
+    above,
 ):
     ndet, nblk, nsub, spans, lanes, rows = sizes
     peers = ndet * nsub
@@ -58,36 +59,40 @@
     det = lax.axis_index("det")
     blk = lax.axis_index("blk")
     sub = lax.axis_index("sub")
-    others = [
-        (db, dd, ds)
-        for dd in range(ndet)
-        for db in range(nblk)
-        for ds in range(nsub)
-        if (db, dd, ds) != (0, 0, 0)
-    ]
-
-    def target(offset):
-        db, dd, ds = offset
-        return {
-            "det": lax.rem(det + dd, ndet),
-            "blk": lax.rem(blk + db, nblk),
-            "sub": lax.rem(sub + ds, nsub),
-        }
-
+    plane_steps = [(db, ds) for db in range(nblk) for ds in range(nsub)]
+    plane = [step for step in plane_steps if step != (0, 0)]
+
+    def beside(step, at=None):
+        place = {"blk": lax.rem(blk + step[0], nblk), "sub": lax.rem(sub + step[1], nsub)}
+        if at is not None:
+            place["det"] = at
+        return place
+
+    def loads_of(names):
+        copies = [pltpu.make_async_copy(a, b, load_sem.at[n]) for n, a, b in names]
+        for copy in copies:
+            copy.start()
+        return copies
+
+    loads = loads_of([(0, tod_hbm, tod_in)])
     barrier = pltpu.get_barrier_semaphore()
-    plane = [offset for offset in others if offset[1] == 0]
-    column = [offset for offset in others if offset[0] == 0 and offset[2] == 0]
-    for offset in plane + column:
-        pl.semaphore_signal(barrier, inc=1, device_id=target(offset), device_id_type=MESH)
-
-    sources = (tod_hbm, pix_hbm, class_hbm, class_weight_hbm, span_block_hbm)
-    landings = (tod_in, pix_in, class_ref, class_weight_ref, span_block_ref)
-    loads = [
-        pltpu.make_async_copy(source, landing, load_sem.at[n])
-        for n, (source, landing) in enumerate(zip(sources, landings))
-    ]
-    for load in loads:
-        load.start()
+
+    def signal(sem, to):
+        pl.semaphore_signal(sem, inc=1, device_id=to, device_id_type=MESH)
+
+    for k in range(ndet - 1, 0, -1):
+        pl.when(det + k < ndet)(lambda k=k: signal(barrier, {"det": det + k}))
+    pl.when(det > 0)(lambda: signal(barrier, {"det": det - 1}))
+    for step in plane:
+        signal(barrier, beside(step))
+    loads += loads_of(
+        [
+            (1, pix_hbm, pix_in),
+            (2, class_hbm, class_ref),
+            (3, class_weight_hbm, class_weight_ref),
+            (4, span_block_hbm, span_block_ref),
+        ]
+    )
 
     part = mine * spans
     loads[0].wait()
@@ -95,6 +100,30 @@
         for span in range(spans):
             stage[seg, pl.ds(span, mine, spans), :] = tod_in[:, seg, span * SPAN : (span + 1) * SPAN]
 
+    def pass_tod(seg):
+        pltpu.make_async_remote_copy(
+            src_ref=stage.at[seg],
+            dst_ref=tod_all.at[det],
+            send_sem=tod_send,
+            recv_sem=tod_recv,
+            device_id={"det": seg},
+            device_id_type=MESH,
+        ).start()
+
+    def reach(k):
+        @pl.when(det + k < ndet)
+        def _():
+            if k > 1:
+                pl.semaphore_wait(above.at[k], 1)
+            pass_tod(det + k)
+            if k + 1 < ndet:
+                pl.when(det > 0)(lambda: signal(above.at[k + 1], {"det": det - 1}))
+
+    pl.semaphore_wait(barrier, len(plane) + det + jnp.where(det + 1 < ndet, 1, 0))
+    for k in range(ndet - 1, 0, -1):
+        pl.when(det >= k)(lambda k=k: pass_tod(det - k))
+    reach(1)
+    tod_all[det] = stage[det]
     loads[2].wait()
     loads[3].wait()
     picked = jnp.zeros((1, detectors), jnp.float32)
@@ -115,20 +144,6 @@
     fine_high_ref[...] = 2.0 * high + upper
     fine_low_ref[...] = low - upper * (lanes // 2)
 
-    pl.semaphore_wait(barrier, len(plane + column))
-    for offset in plane:
-        pl.semaphore_signal(passed, inc=1, device_id=target(offset), device_id_type=MESH)
-    for step in range(1, ndet):
-        seg = lax.rem(det + step, ndet)
-        pltpu.make_async_remote_copy(
-            src_ref=stage.at[seg],
-            dst_ref=tod_all.at[det],
-            send_sem=tod_send,
-            recv_sem=tod_recv,
-            device_id={"det": seg},
-            device_id_type=MESH,
-        ).start()
-    tod_all[det] = stage[det]
     height = peers * TILE
     fine = lanes // 2
     fine_rows = 2 * rows
@@ -188,7 +203,14 @@
         return tuple(new)
 
     start = tuple(jnp.zeros((height, SPAN), jnp.float32) for _ in range(spans))
-    sums = lax.fori_loop(0, detectors // chunk, early_step, start)
+    steps = detectors // chunk
+    sums = lax.fori_loop(0, steps // 2, early_step, start)
+    reach(2)
+    sums = lax.fori_loop(steps // 2, steps, early_step, sums)
+    for k in range(3, ndet):
+        reach(k)
+    for step in plane:
+        signal(passed, beside(step))
     loads[4].wait()
     label_row = lax.broadcasted_iota(jnp.int32, (TILE, SPAN), 0) == 2 * rows
     for span in range(spans):
@@ -197,14 +219,20 @@
             tile = sums[span][p * TILE : (p + 1) * TILE]
             early_out[p, span] = jnp.where(label_row, label, tile)
 
-    slot_of = {offset: n for n, offset in enumerate(others)}
-
-    def send(source, landing, send_sem, recv_sem):
-        for offset in others:
-            to = target(offset)
+    me = (det * nblk + blk) * nsub + sub
+
+    def ranked(j):
+        high = ndet - 1 - j
+        low = jnp.where(j >= det, j + 1, j)
+        return jnp.where(2 * det < ndet, jnp.where(high <= det, high - 1, high), low)
+
+    def send(source, landing, send_sem, recv_sem, count):
+        targets = [beside(step, ranked(j)) for j in range(ndet - 1) for step in plane_steps]
+        targets += [beside(step, det) for step in plane]
+        for to in targets:
             pltpu.make_async_remote_copy(
-                src_ref=source.at[to["det"] * nsub + to["sub"]],
-                dst_ref=landing.at[slot_of[offset]],
+                src_ref=source.at[to["det"] * nsub + to["sub"], *count],
+                dst_ref=landing.at[me, *count],
                 send_sem=send_sem,
                 recv_sem=recv_sem,
                 device_id=to,
@@ -212,13 +240,12 @@
             ).start()
 
     own_place = det * nsub + sub
-    remote = len(others)
-
-    pl.semaphore_wait(passed, len(plane))
-    send(early_out, early_in, early_send, early_recv)
+    remote = total_peers - 1
 
     tod_gone = stage.at[pl.ds(0, ndet - 1)]
     pltpu.make_async_copy(tod_gone, tod_all.at[pl.ds(0, ndet - 1)], tod_recv).wait()
+    pl.semaphore_wait(passed, len(plane))
+    send(early_out, early_in, early_send, early_recv, ())
 
     period = TILE
     folded = jnp.zeros((period, SPAN), jnp.float32)
@@ -253,9 +280,11 @@
     for p in range(peers):
         tiles = [late[span][p * TILE : (p + 1) * TILE] for span in range(spans)]
         late_out[p] = jnp.concatenate(tiles, axis=1)
-    send(late_out, late_in, late_send, late_recv)
-    late_in[remote] = late_out[own_place]
-    early_in[remote] = early_out[own_place]
+    used = (pl.ds(0, fine_rows),)
+    send(late_out, late_in, late_send, late_recv, used)
+    late_in[me] = late_out[own_place]
+    early_in[me] = early_out[own_place]
+    late_bytes = late_in.at[pl.ds(0, remote), *used]
 
     pltpu.make_async_copy(early_in.at[pl.ds(0, remote)], early_in.at[pl.ds(0, remote)], early_recv).wait()
     first = (blk * BLK_OWN).astype(jnp.float32)
@@ -296,7 +325,7 @@
             out_ref[1, b : b + 1, at] = acc[b][r : r + 1, :lanes]
             out_ref[2, b : b + 1, at] = acc[b][rows + r : rows + r + 1, :lanes]
 
-    pltpu.make_async_copy(late_in.at[pl.ds(0, remote)], late_in.at[pl.ds(0, remote)], late_recv).wait()
+    pltpu.make_async_copy(late_bytes, late_bytes, late_recv).wait()
     acc = over_slots(gather_late)
     for b in range(BLK_OWN):
         whole = acc[b]
@@ -310,7 +339,7 @@
 
     pltpu.make_async_copy(tod_gone, tod_all.at[pl.ds(0, ndet - 1)], tod_send).wait()
     pltpu.make_async_copy(early_in.at[pl.ds(0, remote)], early_in.at[pl.ds(0, remote)], early_send).wait()
-    pltpu.make_async_copy(late_in.at[pl.ds(0, remote)], late_in.at[pl.ds(0, remote)], late_send).wait()
+    pltpu.make_async_copy(late_bytes, late_bytes, late_send).wait()
 
 
 def on_device(tod, pixels, span_block, weight_class, class_weight):
@@ -361,6 +390,7 @@
             dma,
             dma,
             pltpu.SemaphoreType.REGULAR,
+            pltpu.SemaphoreType.REGULAR((ndet,)),
         ],
         compiler_params=pltpu.CompilerParams(collective_id=0, has_side_effects=True),
     )(

time: 17.5 us -> 19.6 us (1.12)
  Pallas kernels: 16.1 us -> 18.2 us
    pallas_call x1, Pallas kernels: 16.1 us -> 18.2 us  [on_device(): pl.pallas_call(functools.partial(kernel, (ndet, nblk, nsub, spans, lanes,...]
where the time goes in v1:
time: 19.6 us; the launch traced here: 19.4 us
  Pallas kernels  18.2 us (93%)
  between operations  0.64 us (3%)
  local copies, waits for them, and re-layouts  0.6 us (3%)
    pallas_call x1, Pallas kernels, on_device(): pl.pallas_call(functools.partial(kernel, (ndet, nblk, nsub, spans, lanes,...  18.2 us
    squeeze x1, local copies, waits for them, and re-layouts, on_device(): return (out[0], out[1], out[2])  0.6 us

profile of v1, /device:TPU:0, one launch (start us, length us, event | category | flops | bytes accessed | tf_op | source)
XLA Modules:
  0.0 19.4 jit_solution(15464336085447066598)
XLA Ops:
  0.6 18.2 %shard_map.76 = f32[3,4,384]{2,1,0:T(4,128)S(1)} custom-call(f32[32,4,256]{2,1,0:T(4,128)} %tod_hbm.1, s32[256,128]{1,0:T(8,128)} %bitcast.9, s32[1,128]{1,0:T(1,128)} %bitcast.11, f32[8]{0:T(128)} %class_weight_hbm.1, s32[2,4]{1,0:T(2,128)} %bitcast.10), custom_call_target="tpu_custom_call" | custom-call | tf_op jit(solution)/shard_map/pallas_call | solution.py:362
  18.8 0.6 %slice_bitcast_fusion = (f32[4,384]{1,0:T(4,128)}, f32[4,384]{1,0:T(4,128)}, f32[4,384]{1,0:T(4,128)}) fusion(f32[3,4,384]{2,1,0:T(4,128)S(1)} %shard_map.76), kind=kLoop, calls=%fused_computation | loop fusion | bytes 36864 | tf_op jit(solution)/shard_map/squeeze | solution.py:403

commit v2 on v0

v2 whole, which is shorter than its diff:
```python
import functools

import jax
import jax.numpy as jnp
from jax import lax
from jax.experimental import pallas as pl
from jax.experimental.pallas import tpu as pltpu
from jax.sharding import PartitionSpec as P

BLOCK_PIX = 3072
SPAN = 128
BLK_OWN = 4
TILE = 8
PACK = 16
CHUNK = 96
TIMES = 32
MESH = pl.DeviceIdType.MESH


def kernel(
    sizes,
    tod_hbm,
    pix_hbm,
    class_hbm,
    class_weight_hbm,
    span_block_hbm,
    out_ref,
    class_ref,
    class_weight_ref,
    span_block_ref,
    tod_in,
    pix_in,
    stage,
    tod_all,
    high_ref,
    low_ref,
    turned_high,
    turned_low,
    weight_rows,
    value_ref,
    moment_ref,
    shift_ref,
    near_ref,
    early_out,
    early_in,
    late_out,
    late_in,
    load_sem,
    tod_send,
    tod_recv,
    early_send,
    early_recv,
    late_send,
    late_recv,
    passed,
):
    ndet, nblk, nsub, spans, lanes, rows = sizes
    peers = ndet * nsub
    total_peers = peers * nblk
    mine = tod_hbm.shape[0]
    detectors = ndet * mine
    classes = class_weight_hbm.shape[0]
    det = lax.axis_index("det")
    blk = lax.axis_index("blk")
    sub = lax.axis_index("sub")
    others = [
        (db, dd, ds)
        for dd in range(ndet)
        for db in range(nblk)
        for ds in range(nsub)
        if (db, dd, ds) != (0, 0, 0)
    ]

    def target(offset):
        db, dd, ds = offset
        return {
            "det": lax.rem(det + dd, ndet),
            "blk": lax.rem(blk + db, nblk),
            "sub": lax.rem(sub + ds, nsub),
        }

    barrier = pltpu.get_barrier_semaphore()
    plane = [offset for offset in others if offset[1] == 0]
    column = [offset for offset in others if offset[0] == 0 and offset[2] == 0]
    for offset in plane + column:
        pl.semaphore_signal(barrier, inc=1, device_id=target(offset), device_id_type=MESH)

    sources = (tod_hbm, pix_hbm, class_hbm, class_weight_hbm, span_block_hbm)
    landings = (tod_in, pix_in, class_ref, class_weight_ref, span_block_ref)
    loads = [
        pltpu.make_async_copy(source, landing, load_sem.at[n])
        for n, (source, landing) in enumerate(zip(sources, landings))
    ]
    for load in loads:
        load.start()

    part = mine * spans
    height = peers * TILE
    fine = lanes // 2
    fine_rows = 2 * rows
    field = SPAN // spans

    loads[0].wait()
    for seg in range(ndet):
        for span in range(spans):
            stage[seg, pl.ds(span, mine, spans), :] = tod_in[:, seg, span * SPAN : (span + 1) * SPAN]

    pl.semaphore_wait(barrier, len(plane + column))
    for high in range(ndet - 1, 0, -1):
        seg = jnp.where(high > det, high, high - 1)
        seg = jnp.where((det == 0) & (seg < ndet - 1), ndet - 1 - seg, seg)
        pltpu.make_async_remote_copy(
            src_ref=stage.at[seg],
            dst_ref=tod_all.at[det],
            send_sem=tod_send,
            recv_sem=tod_recv.at[det],
            device_id={"det": seg},
            device_id_type=MESH,
        ).start()
    for offset in plane:
        pl.semaphore_signal(passed, inc=1, device_id=target(offset), device_id_type=MESH)
    tod_all[det] = stage[det]

    loads[2].wait()
    loads[3].wait()
    picked = jnp.zeros((1, detectors), jnp.float32)
    for c in range(classes):
        picked = jnp.where(class_ref[...] == c, class_weight_ref[c], picked)
    turned = jnp.transpose(jnp.broadcast_to(picked, (SPAN, detectors)))
    for span in range(spans):
        weight_rows[pl.ds(span, detectors, spans), :] = turned

    def place(pixel):
        high = jnp.floor((pixel + 0.5) * (1.0 / fine))
        return high, pixel - high * fine

    loads[1].wait()
    high_ref[...], low_ref[...] = place(pix_in[...].astype(jnp.float32))
    for span in range(spans):
        across = jnp.transpose(pix_in[pl.ds(span, detectors, spans), :].astype(jnp.float32))
        turned_high[span], turned_low[span] = place(across)

    def to_low(x):
        return x.astype(jnp.float32).astype(jnp.bfloat16)

    def ids_of(width):
        def iota(tile):
            return lax.broadcasted_iota(jnp.int32, (PACK, width), 0) + tile * PACK

        low = [to_low(iota(t)) for t in range(field // PACK)]
        high = []
        for t in range(height // PACK):
            within = iota(t) % TILE
            high.append(to_low(jnp.where(within < fine_rows, iota(t) // TILE * fine_rows + within, -1)))
        one = jnp.ones((PACK, width), jnp.bfloat16)
        return low, high, one, jnp.zeros((PACK, width), jnp.bfloat16)

    def hot(ids, where, filled, zero):
        return jnp.concatenate([jnp.where(i == where, filled, zero) for i in ids], axis=0)

    def contract(left, right):
        return lax.dot_general(left, right, (((1,), (1,)), ((), ())), preferred_element_type=jnp.float32)

    low_ids, high_ids, one, zero = ids_of(detectors)
    blank = jnp.zeros((field, detectors), jnp.bfloat16)
    weight_low = jnp.broadcast_to(picked, (PACK, detectors)).astype(jnp.bfloat16)
    times = min(TIMES, SPAN)

    def early_step(i, sums):
        base = pl.multiple_of(i * times, times)
        for n in range(times):
            left, right = [], []
            for span in range(spans):

                def across(ref):
                    return jnp.broadcast_to(ref[span, pl.ds(base + n, 1), :], (PACK, detectors)).astype(jnp.bfloat16)

                hit = hot(low_ids, across(turned_low), one, zero)
                right.append(jnp.concatenate([hit if s == span else blank for s in range(spans)], axis=0))
                where = across(turned_high)
                left.append(
                    jnp.concatenate(
                        [hot(high_ids, where, weight_low, zero), hot(high_ids, where, one, zero)], axis=0
                    )
                )
            new = contract(jnp.concatenate(left, axis=1), jnp.concatenate(right, axis=1))
            moment_ref[base + n] = new[:height]
            sums = sums + new
        return sums

    sums = lax.fori_loop(0, SPAN // times, early_step, jnp.zeros((2 * height, SPAN), jnp.float32))

    lane = lax.broadcasted_iota(jnp.int32, (TILE, SPAN), 1)
    label_row = lax.broadcasted_iota(jnp.int32, (TILE, SPAN), 0) == fine_rows
    loads[4].wait()
    label = jnp.zeros((TILE, SPAN), jnp.float32)
    for span in range(spans):
        label = jnp.where(lane >= span * field, span_block_ref[span, det].astype(jnp.float32), label)
    for p in range(peers):
        early_out[p, 0] = jnp.where(label_row, label, sums[p * TILE : (p + 1) * TILE])
        early_out[p, 1] = sums[height + p * TILE : height + (p + 1) * TILE]

    slot_of = {offset: n for n, offset in enumerate(others)}

    def send(source, landing, send_sem, recv_sem, count):
        for offset in others:
            to = target(offset)
            pltpu.make_async_remote_copy(
                src_ref=source.at[to["det"] * nsub + to["sub"], *count],
                dst_ref=landing.at[slot_of[offset], *count],
                send_sem=send_sem,
                recv_sem=recv_sem,
                device_id=to,
                device_id_type=MESH,
            ).start()

    own_place = det * nsub + sub
    remote = len(others)

    pl.semaphore_wait(passed, len(plane))
    send(early_out, early_in, early_send, early_recv, ())

    far = jnp.where(det > 0, 0, ndet - 1)
    first_near = jnp.where(det > 0, 1, 0)

    def arrived(q):
        pltpu.make_async_copy(stage.at[0], tod_all.at[q], tod_recv.at[q]).wait()

    def rows_of(q):
        return pl.ds(pl.multiple_of(q * part, TILE), part)

    def fold(total, q):
        weighted = tod_all[q] * weight_rows[rows_of(q), :]
        for k in range(part // TILE):
            total = total + weighted[k * TILE : (k + 1) * TILE]
        return total

    def over_spans(folded):
        shift = spans
        while shift < TILE:
            folded = folded + pltpu.roll(folded, shift, 0)
            shift *= 2
        return folded

    def form(q, level):
        repeated = jnp.concatenate([level] * (part // TILE), axis=0)
        value_ref[rows_of(q), :] = weight_rows[rows_of(q), :] * (tod_all[q] - repeated)

    near = [first_near + k for k in range(ndet - 1)]
    folded = jnp.zeros((TILE, SPAN), jnp.float32)
    for q in near:
        pl.when(q != det)(functools.partial(arrived, q))
        folded = fold(folded, q)
    source = lax.broadcasted_iota(jnp.int32, (1, detectors), 1) // mine
    near_total = jnp.sum(jnp.where(source == far, 0.0, picked), axis=1, keepdims=True)
    total = jnp.sum(picked, axis=1, keepdims=True)
    level = over_spans(folded) / near_total
    for q in near:
        form(q, level)

    row_low, row_high, row_one, row_zero = ids_of(SPAN)

    def spread(ref, row):
        return jnp.broadcast_to(ref[pl.ds(row, 1), :], (PACK, SPAN)).astype(jnp.bfloat16)

    def value_sums(first, count, sums):
        base = pl.multiple_of(first * spans, TILE)
        new = []
        for span in range(spans):
            left, right = [], []
            for d in range(count):
                r = base + d * spans + span
                right.append(hot(row_low, spread(low_ref, r), row_one, row_zero))
                left.append(hot(row_high, spread(high_ref, r), spread(value_ref, r), row_zero))
            both = contract(jnp.concatenate(left, axis=1), jnp.concatenate(right, axis=1))
            new.append(sums[span] + both)
        return tuple(new)

    nearby = (ndet - 1) * mine
    chunk = max(c for c in range(mine, CHUNK + 1, mine) if nearby % c == 0)
    start = tuple(jnp.zeros((height, field), jnp.float32) for _ in range(spans))
    late = lax.fori_loop(
        0,
        nearby // chunk,
        lambda i, sums: value_sums(first_near * mine + i * chunk, chunk, sums),
        start,
    )

    near_ref[...] = jnp.concatenate(late, axis=1)
    arrived(far)
    folded = fold(folded, far)
    form(far, level)
    change = over_spans(folded) / total - level
    by_lane = [jnp.broadcast_to(change[span : span + 1], (field, SPAN)) for span in range(spans)]
    shift_ref[...] = jnp.transpose(jnp.concatenate(by_lane, axis=0))
    late = value_sums(far * mine, mine, start)
    signal = near_ref[...] + jnp.concatenate(late, axis=1)
    moved = [jnp.zeros((height, SPAN), jnp.float32) for _ in range(2)]
    for t in range(SPAN):
        by = jnp.broadcast_to(shift_ref[t : t + 1, :], (height, SPAN))
        moved[t % 2] = moved[t % 2] + by * moment_ref[t]
    signal = signal - (moved[0] + moved[1])
    for p in range(peers):
        late_out[p] = signal[p * TILE : (p + 1) * TILE]
    used = (pl.ds(0, fine_rows),)
    send(late_out, late_in, late_send, late_recv, used)
    late_in[remote] = late_out[own_place]
    early_in[remote] = early_out[own_place]

    def finish(copy_sem, landing):
        pltpu.make_async_copy(landing, landing, copy_sem).wait()

    early_all = early_in.at[pl.ds(0, remote)]
    late_all = late_in.at[pl.ds(0, remote), *used]
    first = (blk * BLK_OWN).astype(jnp.float32)

    def gather(tiles_of):
        def step(n, acc):
            label = jnp.broadcast_to(early_in[n, 0, pl.ds(fine_rows, 1), :], (TILE, SPAN))
            acc = list(acc)
            for b in range(BLK_OWN):
                mine_here = label == first + b
                for k, tile in enumerate(tiles_of(n)):
                    at = k * BLK_OWN + b
                    acc[at] = acc[at] + jnp.where(mine_here, tile, 0.0)
            return tuple(acc)

        kinds = len(tiles_of(0))
        acc = tuple(jnp.zeros((TILE, SPAN), jnp.float32) for _ in range(kinds * BLK_OWN))
        if total_peers <= 16:
            for n in range(total_peers):
                acc = step(n, acc)
            return acc
        return lax.fori_loop(0, total_peers, step, acc)

    def put(kind, tiles):
        for b, tile in enumerate(tiles):
            whole = tile
            for span in range(1, spans):
                whole = whole + pltpu.roll(tile, span * field, 1)
            for r in range(fine_rows):
                skip = r * fine % SPAN // field * field
                skip = skip if skip + fine <= SPAN else 0
                line = whole[r : r + 1, skip : skip + fine]
                out_ref[kind, b : b + 1, r * fine : (r + 1) * fine] = line

    finish(early_recv, early_all)
    acc = gather(lambda n: (early_in[n, 0], early_in[n, 1]))
    put(1, acc[:BLK_OWN])
    put(2, acc[BLK_OWN:])

    finish(late_recv, late_all)
    put(0, gather(lambda n: (late_in[n],)))

    tod_gone = tod_all.at[pl.ds(0, ndet - 1)]
    finish(tod_send, tod_gone)
    finish(early_send, early_all)
    finish(late_send, late_all)


def on_device(tod, pixels, span_block, weight_class, class_weight):
    ndet, nblk, nsub = (lax.axis_size(a) for a in ("det", "blk", "sub"))
    mine, segments, samples = tod.shape
    detectors = pixels.shape[0]
    spans = samples // SPAN
    peers = ndet * nsub
    slots = peers * nblk
    width = BLOCK_PIX // peers
    lanes = next(n for n in range(SPAN, 0, -1) if width % n == 0)
    rows = width // lanes
    assert segments == ndet and detectors == ndet * mine
    assert TILE % spans == 0 and 2 * rows < TILE and lanes % 2 == 0 and lanes // 2 <= SPAN // spans
    flat = (detectors * spans, SPAN)
    vmem = pl.BlockSpec(memory_space=pltpu.VMEM)
    hbm = pl.BlockSpec(memory_space=pl.ANY)
    f32 = jnp.float32
    dma = pltpu.SemaphoreType.DMA
    out = pl.pallas_call(
        functools.partial(kernel, (ndet, nblk, nsub, spans, lanes, rows)),
        out_shape=pltpu.VMEM((3, BLK_OWN, width), f32),
        in_specs=[hbm] * 5,
        out_specs=vmem,
        scratch_shapes=[
            pltpu.VMEM((1, detectors), jnp.int32),
            pltpu.SMEM(class_weight.shape, f32),
            pltpu.SMEM((spans, segments), jnp.int32),
            pltpu.VMEM(tod.shape, f32),
            pltpu.VMEM(flat, jnp.int32),
            pltpu.VMEM((ndet, mine * spans, SPAN), f32),
            pltpu.VMEM((ndet, mine * spans, SPAN), f32),
            pltpu.VMEM(flat, f32),
            pltpu.VMEM(flat, f32),
            pltpu.VMEM((spans, SPAN, detectors), f32),
            pltpu.VMEM((spans, SPAN, detectors), f32),
            pltpu.VMEM(flat, f32),
            pltpu.VMEM(flat, f32),
            pltpu.VMEM((SPAN, peers * TILE, SPAN), f32),
            pltpu.VMEM((SPAN, SPAN), f32),
            pltpu.VMEM((peers * TILE, SPAN), f32),
            pltpu.VMEM((peers, 2, TILE, SPAN), f32),
            pltpu.VMEM((slots, 2, TILE, SPAN), f32),
            pltpu.VMEM((peers, TILE, SPAN), f32),
            pltpu.VMEM((slots, TILE, SPAN), f32),
            dma((5,)),
            dma,
            dma((ndet,)),
            dma,
            dma,
            dma,
            dma,
            pltpu.SemaphoreType.REGULAR,
        ],
        compiler_params=pltpu.CompilerParams(collective_id=0, has_side_effects=True),
    )(
        tod,
        pixels.reshape(flat),
        weight_class.reshape(1, detectors),
        class_weight,
        span_block.T,
    )
    return (out[0], out[1], out[2])


def solution(mesh):
    placed = (
        P(("groups", "det"), None, ("blk", "sub")),
        P("groups", "det", ("blk", "sub")),
        P("groups", ("blk", "sub")),
        P("groups"),
        P("groups"),
    )
    sliced = P(("groups", "blk"), ("det", "sub"))
    return jax.shard_map(
        on_device,
        mesh=mesh,
        in_specs=placed,
        out_specs=(sliced, sliced, sliced),
        check_vma=False,
    )
```

time: 17.5 us -> 16.4 us (0.937)
  Pallas kernels: 16.1 us -> 15 us
    pallas_call x1, Pallas kernels: 16.1 us -> 15 us  [on_device(): pl.pallas_call(functools.partial(kernel, (ndet, nblk, nsub, spans, lanes,...]
where the time goes in v2:
time: 16.4 us; the launch traced here: 16.2 us
  Pallas kernels  15 us (91%)
  between operations  0.64 us (4%)
  local copies, waits for them, and re-layouts  0.6 us (4%)
    pallas_call x1, Pallas kernels, on_device(): pl.pallas_call(functools.partial(kernel, (ndet, nblk, nsub, spans, lanes,...  15 us
    squeeze x1, local copies, waits for them, and re-layouts, on_device(): return (out[0], out[1], out[2])  0.6 us

profile of v2, /device:TPU:0, one launch (start us, length us, event | category | flops | bytes accessed | tf_op | source)
XLA Modules:
  0.0 16.2 jit_solution(421923338900531752)
XLA Ops:
  0.6 15.0 %shard_map.76 = f32[3,4,384]{2,1,0:T(4,128)S(1)} custom-call(f32[32,4,256]{2,1,0:T(4,128)} %tod_hbm.1, s32[256,128]{1,0:T(8,128)} %bitcast.9, s32[1,128]{1,0:T(1,128)} %bitcast.11, f32[8]{0:T(128)} %class_weight_hbm.1, s32[2,4]{1,0:T(2,128)} %bitcast.10), custom_call_target="tpu_custom_call" | custom-call | tf_op jit(solution)/shard_map/pallas_call | solution.py:378
  15.6 0.6 %slice_bitcast_fusion = (f32[4,384]{1,0:T(4,128)}, f32[4,384]{1,0:T(4,128)}, f32[4,384]{1,0:T(4,128)}) fusion(f32[3,4,384]{2,1,0:T(4,128)S(1)} %shard_map.76), kind=kLoop, calls=%fused_computation | loop fusion | bytes 36864 | tf_op jit(solution)/shard_map/squeeze | solution.py:421

commit v3 on v2

v3 whole, which is shorter than its diff:
```python
import functools

import jax
import jax.numpy as jnp
from jax import lax
from jax.experimental import pallas as pl
from jax.experimental.pallas import tpu as pltpu
from jax.sharding import PartitionSpec as P

BLOCK_PIX = 3072
SPAN = 128
BLK_OWN = 4
TILE = 8
PACK = 16
EARLY = 64
LATE = 128
MESH = pl.DeviceIdType.MESH


def kernel(
    sizes,
    tod_hbm,
    pix_hbm,
    class_hbm,
    class_weight_hbm,
    span_block_hbm,
    out_ref,
    class_ref,
    class_weight_ref,
    span_block_ref,
    pix_in,
    stage,
    tod_all,
    high_ref,
    low_ref,
    weight_rows,
    value_ref,
    early_flat,
    held,
    early_out,
    early_in,
    late_out,
    late_in,
    load_sem,
    tod_send,
    tod_recv,
    early_send,
    early_recv,
    late_send,
    late_recv,
    passed,
):
    ndet, nblk, nsub, spans, lanes, rows = sizes
    peers = ndet * nsub
    total_peers = peers * nblk
    mine = tod_hbm.shape[0]
    detectors = ndet * mine
    classes = class_weight_hbm.shape[0]
    det = lax.axis_index("det")
    blk = lax.axis_index("blk")
    sub = lax.axis_index("sub")
    others = [
        (db, dd, ds)
        for dd in range(ndet)
        for db in range(nblk)
        for ds in range(nsub)
        if (db, dd, ds) != (0, 0, 0)
    ]

    def target(offset):
        db, dd, ds = offset
        return {
            "det": lax.rem(det + dd, ndet),
            "blk": lax.rem(blk + db, nblk),
            "sub": lax.rem(sub + ds, nsub),
        }

    for seg in range(ndet):
        for span in range(spans):
            pltpu.make_async_copy(
                tod_hbm.at[:, seg, pl.ds(span * SPAN, SPAN)], stage.at[seg, span], load_sem.at[0]
            ).start()

    barrier = pltpu.get_barrier_semaphore()
    plane = [offset for offset in others if offset[1] == 0]
    column = [offset for offset in others if offset[0] == 0 and offset[2] == 0]
    for offset in column + plane:
        pl.semaphore_signal(barrier, inc=1, device_id=target(offset), device_id_type=MESH)

    sources = (pix_hbm, class_hbm, class_weight_hbm, span_block_hbm)
    landings = (pix_in, class_ref, class_weight_ref, span_block_ref)
    loads = [
        pltpu.make_async_copy(source, landing, load_sem.at[n + 1])
        for n, (source, landing) in enumerate(zip(sources, landings))
    ]
    for load in loads:
        load.start()

    height = peers * TILE
    group = 4 * rows
    tall = -(-peers * group // PACK) * PACK
    fine = lanes // 2
    fine_rows = 2 * rows
    field = SPAN // spans

    pltpu.make_async_copy(stage, stage, load_sem.at[0]).wait()
    pl.semaphore_wait(barrier, len(plane + column))
    for span in range(spans):
        for high in range(ndet - 1, 0, -1):
            seg = jnp.where(high > det, high, high - 1)
            seg = jnp.where((det == 0) & (seg < ndet - 1), ndet - 1 - seg, seg)
            pltpu.make_async_remote_copy(
                src_ref=stage.at[seg, span],
                dst_ref=tod_all.at[det, span],
                send_sem=tod_send,
                recv_sem=tod_recv.at[span],
                device_id={"det": seg},
                device_id_type=MESH,
            ).start()
    for offset in plane:
        pl.semaphore_signal(passed, inc=1, device_id=target(offset), device_id_type=MESH)
    tod_all[det] = stage[det]

    loads[1].wait()
    loads[2].wait()
    picked = jnp.zeros((1, detectors), jnp.float32)
    for c in range(classes):
        picked = jnp.where(class_ref[...] == c, class_weight_ref[c], picked)
    weight_rows[...] = jnp.transpose(jnp.broadcast_to(picked, (SPAN, detectors)))

    def place(pixel):
        high = jnp.floor((pixel + 0.5) * (1.0 / fine))
        return high, pixel - high * fine

    loads[0].wait()
    for span in range(spans):
        pixel = pix_in[pl.ds(span, detectors, spans), :].astype(jnp.float32)
        high_ref[span], low_ref[span] = place(pixel)

    def to_low(x):
        return x.astype(jnp.float32).astype(jnp.bfloat16)

    def iota(tile):
        return lax.broadcasted_iota(jnp.int32, (PACK, SPAN), 0) + tile * PACK

    low_ids = [to_low(iota(t)) for t in range(field // PACK)]
    high_ids = []
    for t in range(height // PACK):
        within = iota(t) % TILE
        high_ids.append(to_low(jnp.where(within < fine_rows, iota(t) // TILE * fine_rows + within, -1)))
    both_ids = []
    is_weight = {}
    for t in range(tall // PACK):
        peer = iota(t) // group
        both_ids.append(to_low(jnp.where(peer < peers, peer * fine_rows + iota(t) % fine_rows, -1)))
        is_weight[t * PACK % group] = to_low(jnp.where(iota(t) % group < fine_rows, 1, 0)) > 0.5
    one = jnp.ones((PACK, SPAN), jnp.bfloat16)
    zero = jnp.zeros((PACK, SPAN), jnp.bfloat16)

    def hot(ids, where, filled):
        return jnp.concatenate([jnp.where(i == where, f, zero) for i, f in zip(ids, filled)], axis=0)

    def spread(ref, row):
        return jnp.broadcast_to(ref[pl.ds(row, 1), :], (PACK, SPAN)).astype(jnp.bfloat16)

    def contract(left, right):
        return lax.dot_general(
            jnp.concatenate(left, axis=1),
            jnp.concatenate(right, axis=1),
            (((1,), (1,)), ((), ())),
            preferred_element_type=jnp.float32,
        )

    ones = [one] * len(low_ids)
    chunk = min(EARLY, detectors)

    def early_step(i, sums):
        base = pl.multiple_of(i * chunk, TILE)
        new = []
        for span in range(spans):
            left, right = [], []
            for d in range(chunk):
                right.append(hot(low_ids, spread(low_ref.at[span], base + d), ones))
                weight = spread(weight_rows, base + d)
                mixed = {k: jnp.where(mask, weight, one) for k, mask in is_weight.items()}
                filled = [mixed[t * PACK % group] for t in range(len(both_ids))]
                left.append(hot(both_ids, spread(high_ref.at[span], base + d), filled))
            new.append(sums[span] + contract(left, right))
        return tuple(new)

    start = tuple(jnp.zeros((tall, field), jnp.float32) for _ in range(spans))
    sums = lax.fori_loop(0, detectors // chunk, early_step, start)
    early_flat[...] = jnp.concatenate(sums, axis=1)

    lane = lax.broadcasted_iota(jnp.int32, (1, SPAN), 1)
    loads[3].wait()
    label = jnp.zeros((1, SPAN), jnp.float32)
    for span in range(spans):
        label = jnp.where(lane >= span * field, span_block_ref[span, det].astype(jnp.float32), label)
    for p in range(peers):
        early_out[p, :group] = early_flat[p * group : (p + 1) * group]
        early_out[p, group : group + 1] = label

    slot_of = {offset: n for n, offset in enumerate(others)}

    def send(source, landing, send_sem, recv_sem, count):
        for offset in others:
            to = target(offset)
            pltpu.make_async_remote_copy(
                src_ref=source.at[to["det"] * nsub + to["sub"], *count],
                dst_ref=landing.at[slot_of[offset], *count],
                send_sem=send_sem,
                recv_sem=recv_sem,
                device_id=to,
                device_id_type=MESH,
            ).start()

    own_place = det * nsub + sub
    remote = len(others)

    pl.semaphore_wait(passed, len(plane))
    early_used = (pl.ds(0, group + 1),)
    send(early_out, early_in, early_send, early_recv, early_used)

    total = jnp.sum(picked, axis=1, keepdims=True)
    late_chunk = min(LATE, detectors)

    def value_sums(span, i, sums):
        base = pl.multiple_of(i * late_chunk, TILE)
        new = []
        for half in range(2):
            left, right = [], []
            for n in range(late_chunk // 2):
                d = base + half * (late_chunk // 2) + n
                right.append(hot(low_ids, spread(low_ref.at[span], d), ones))
                value = spread(value_ref.at[span], d)
                left.append(hot(high_ids, spread(high_ref.at[span], d), [value] * len(high_ids)))
            new.append(sums[half] + contract(left, right))
        return tuple(new)

    def arrived(span):
        gone = tod_all.at[pl.ds(0, ndet - 1), span]
        pltpu.make_async_copy(gone, gone, tod_recv.at[span]).wait()

    for span in range(spans):
        arrived(span)
        folded = jnp.zeros((TILE, SPAN), jnp.float32)
        for q in range(ndet):
            weighted = tod_all[q, span] * weight_rows[q * mine : (q + 1) * mine]
            for k in range(mine // TILE):
                folded = folded + weighted[k * TILE : (k + 1) * TILE]
        shift = 1
        while shift < TILE:
            folded = folded + pltpu.roll(folded, shift, 0)
            shift *= 2
        repeated = jnp.concatenate([folded / total] * (mine // TILE), axis=0)
        for q in range(ndet):
            piece = slice(q * mine, (q + 1) * mine)
            clean = tod_all[q, span] - repeated
            if q * mine % late_chunk >= late_chunk // 2:
                clean = repeated - tod_all[q, span]
            value_ref[span, piece] = weight_rows[piece] * clean
        halves = lax.fori_loop(
            0,
            detectors // late_chunk,
            functools.partial(value_sums, span),
            tuple(jnp.zeros((height, field), jnp.float32) for _ in range(2)),
        )
        held[span] = halves[0] - halves[1]
    signal = jnp.concatenate([held[span] for span in range(spans)], axis=1)
    for p in range(peers):
        late_out[p] = signal[p * TILE : (p + 1) * TILE]
    used = (pl.ds(0, fine_rows),)
    send(late_out, late_in, late_send, late_recv, used)
    late_in[remote] = late_out[own_place]
    early_in[remote] = early_out[own_place]

    def finish(copy_sem, landing):
        pltpu.make_async_copy(landing, landing, copy_sem).wait()

    early_all = early_in.at[pl.ds(0, remote), *early_used]
    late_all = late_in.at[pl.ds(0, remote), *used]
    first = (blk * BLK_OWN).astype(jnp.float32)

    def gather(tiles_of):
        def step(n, acc):
            label = jnp.broadcast_to(early_in[n, pl.ds(group, 1), :], (TILE, SPAN))
            acc = list(acc)
            for b in range(BLK_OWN):
                mine_here = label == first + b
                for k, tile in enumerate(tiles_of(n)):
                    at = k * BLK_OWN + b
                    acc[at] = acc[at] + jnp.where(mine_here, tile, 0.0)
            return tuple(acc)

        kinds = len(tiles_of(0))
        acc = tuple(jnp.zeros((TILE, SPAN), jnp.float32) for _ in range(kinds * BLK_OWN))
        if total_peers <= 16:
            for n in range(total_peers):
                acc = step(n, acc)
            return acc
        return lax.fori_loop(0, total_peers, step, acc)

    def put(kind, tiles, top=0):
        for b, tile in enumerate(tiles):
            whole = tile
            for span in range(1, spans):
                whole = whole + pltpu.roll(tile, span * field, 1)
            for r in range(fine_rows):
                skip = r * fine % SPAN // field * field
                skip = skip if skip + fine <= SPAN else 0
                line = whole[top + r : top + r + 1, skip : skip + fine]
                out_ref[kind, b : b + 1, r * fine : (r + 1) * fine] = line

    finish(early_recv, early_all)
    acc = gather(lambda n: (early_in[n, :TILE], early_in[n, TILE:]))
    tiles = [jnp.concatenate([acc[b], acc[BLK_OWN + b]], axis=0) for b in range(BLK_OWN)]
    put(1, tiles)
    put(2, tiles, fine_rows)

    finish(late_recv, late_all)
    put(0, gather(lambda n: (late_in[n],)))

    tod_gone = tod_all.at[pl.ds(0, ndet - 1)]
    finish(tod_send, tod_gone)
    finish(early_send, early_all)
    finish(late_send, late_all)


def on_device(tod, pixels, span_block, weight_class, class_weight):
    ndet, nblk, nsub = (lax.axis_size(a) for a in ("det", "blk", "sub"))
    mine, segments, samples = tod.shape
    detectors = pixels.shape[0]
    spans = samples // SPAN
    peers = ndet * nsub
    slots = peers * nblk
    width = BLOCK_PIX // peers
    lanes = next(n for n in range(SPAN, 0, -1) if width % n == 0)
    rows = width // lanes
    assert segments == ndet and detectors == ndet * mine
    assert TILE % spans == 0 and 2 * rows < TILE and lanes % 2 == 0 and lanes // 2 <= SPAN // spans
    flat = (detectors * spans, SPAN)
    vmem = pl.BlockSpec(memory_space=pltpu.VMEM)
    hbm = pl.BlockSpec(memory_space=pl.ANY)
    f32 = jnp.float32
    dma = pltpu.SemaphoreType.DMA
    out = pl.pallas_call(
        functools.partial(kernel, (ndet, nblk, nsub, spans, lanes, rows)),
        out_shape=pltpu.VMEM((3, BLK_OWN, width), f32),
        in_specs=[hbm] * 5,
        out_specs=vmem,
        scratch_shapes=[
            pltpu.VMEM((1, detectors), jnp.int32),
            pltpu.SMEM(class_weight.shape, f32),
            pltpu.SMEM((spans, segments), jnp.int32),
            pltpu.VMEM(flat, jnp.int32),
            pltpu.VMEM((ndet, spans, mine, SPAN), f32),
            pltpu.VMEM((ndet, spans, mine, SPAN), f32),
            pltpu.VMEM((spans, detectors, SPAN), f32),
            pltpu.VMEM((spans, detectors, SPAN), f32),
            pltpu.VMEM((detectors, SPAN), f32),
            pltpu.VMEM((spans, detectors, SPAN), f32),
            pltpu.VMEM((-(-peers * 4 * rows // PACK) * PACK, SPAN), f32),
            pltpu.VMEM((spans, peers * TILE, SPAN // spans), f32),
            pltpu.VMEM((peers, PACK, SPAN), f32),
            pltpu.VMEM((slots, PACK, SPAN), f32),
            pltpu.VMEM((peers, TILE, SPAN), f32),
            pltpu.VMEM((slots, TILE, SPAN), f32),
            dma((5,)),
            dma,
            dma((spans,)),
            dma,
            dma,
            dma,
            dma,
            pltpu.SemaphoreType.REGULAR,
        ],
        compiler_params=pltpu.CompilerParams(collective_id=0, has_side_effects=True),
    )(
        tod,
        pixels.reshape(flat),
        weight_class.reshape(1, detectors),
        class_weight,
        span_block.T,
    )
    return (out[0], out[1], out[2])


def solution(mesh):
    placed = (
        P(("groups", "det"), None, ("blk", "sub")),
        P("groups", "det", ("blk", "sub")),
        P("groups", ("blk", "sub")),
        P("groups"),
        P("groups"),
    )
    sliced = P(("groups", "blk"), ("det", "sub"))
    return jax.shard_map(
        on_device,
        mesh=mesh,
        in_specs=placed,
        out_specs=(sliced, sliced, sliced),
        check_vma=False,
    )
```

time: 16.4 us -> 16.4 us (level)
  no operation moved by 1% of the time
where the time goes in v3:
time: 16.4 us; the launch traced here: 16.2 us
  Pallas kernels  15 us (91%)
  between operations  0.64 us (4%)
  local copies, waits for them, and re-layouts  0.6 us (4%)
    pallas_call x1, Pallas kernels, on_device(): pl.pallas_call(functools.partial(kernel, (ndet, nblk, nsub, spans, lanes,...  15 us
    squeeze x1, local copies, waits for them, and re-layouts, on_device(): return (out[0], out[1], out[2])  0.6 us

profile of v3, /device:TPU:0, one launch (start us, length us, event | category | flops | bytes accessed | tf_op | source)
XLA Modules:
  0.0 16.2 jit_solution(2754187345020889051)
XLA Ops:
  0.6 15.0 %shard_map.76 = f32[3,4,384]{2,1,0:T(4,128)S(1)} custom-call(f32[32,4,256]{2,1,0:T(4,128)} %tod_hbm.1, s32[256,128]{1,0:T(8,128)} %bitcast.9, s32[1,128]{1,0:T(1,128)} %bitcast.11, f32[8]{0:T(128)} %class_weight_hbm.1, s32[2,4]{1,0:T(2,128)} %bitcast.10), custom_call_target="tpu_custom_call" | custom-call | tf_op jit(solution)/shard_map/pallas_call | solution.py:347
  15.6 0.6 %slice_bitcast_fusion = (f32[4,384]{1,0:T(4,128)}, f32[4,384]{1,0:T(4,128)}, f32[4,384]{1,0:T(4,128)}) fusion(f32[3,4,384]{2,1,0:T(4,128)S(1)} %shard_map.76), kind=kLoop, calls=%fused_computation | loop fusion | bytes 36864 | tf_op jit(solution)/shard_map/squeeze | solution.py:386
